TPU v7x, 32 devices: a 4x4x1 block of a 4x4x8 slice. The times are simulated.
32 devices in a mesh: batch: 1 (over z), col: 32 (over y, x, core).
Axes of the slice: x: 4, y: 4, z: 1, core: 2. Of those that a mesh axis runs over, the one named last changes fastest.
The devices are a block of a 4x4x8 slice.
Arguments:
- lower: bfloat16 [8192, 8192], P('batch', 'col')
- rhs: bfloat16 [8192, 32768], P('batch', 'col')
Outputs:
- output: bfloat16 [8192, 32768], P('batch', 'col')
All inputs are finite; a program needn't handle non-finite values.
Results may differ from a plain program's by a relative error of at most 0.001.
Values are sent between devices in bfloat16 or wider.
A program may use at most 768 MiB of HBM per device.

v0:
```python
import jax
import jax.numpy as jnp
from jax import lax
from jax.sharding import PartitionSpec as P

BLOCK_SIZE = 256


def solution(mesh):
    group_size = mesh.shape["col"]

    def local_product(l_cols, b_cols):
        mat_order, local_width = l_cols.shape
        per_dev = local_width // BLOCK_SIZE
        super_width = group_size * BLOCK_SIZE
        pieces = [l_cols[panel_idx * super_width:, panel_idx * BLOCK_SIZE:(panel_idx + 1) * BLOCK_SIZE] for panel_idx in range(per_dev)]
        packed = jnp.concatenate(pieces, axis=0)
        gathered = lax.all_gather(packed, "col")
        col_bands = []
        offset = 0
        for panel_idx in range(per_dev):
            band_rows = mat_order - panel_idx * super_width
            panel_band = gathered[:, offset:offset + band_rows, :]
            offset = offset + band_rows
            panel_band = jnp.transpose(panel_band, (1, 0, 2)).reshape(band_rows, super_width)
            col_bands.append(jnp.pad(panel_band, ((panel_idx * super_width, 0), (0, 0))))
        natural = jnp.concatenate(col_bands, axis=1)
        out_rows = []
        for row_idx in range(mat_order // BLOCK_SIZE):
            row_end = (row_idx + 1) * BLOCK_SIZE
            strip = natural[row_idx * BLOCK_SIZE:row_end, :row_end]
            block_out = jnp.dot(strip, b_cols[:row_end], preferred_element_type=jnp.float32)
            out_rows.append(block_out.astype(jnp.bfloat16))
        return jnp.concatenate(out_rows, axis=0)

    return jax.shard_map(local_product, mesh=mesh, in_specs=(P("batch", "col"), P("batch", "col")), out_specs=P("batch", "col"), check_vma=False)
```

profile of v0, /device:TPU:97, one launch (start us, length us, event | category | flops | bytes accessed | tf_op | source)
XLA Modules:
  0.0 730.2 jit_solution(13519321108205820002)
XLA Ops:
  7.3 376.9 %all-gather.3.cloned.1.call-done = bf16[262144,256]{1,0:T(8,128)(2,1)} async-done(((bf16[8192,256]{1,0:T(8,128)(2,1)}), bf16[262144,256]{1,0:T(8,128)(2,1)}) %all-gather.3.cloned.1.call-update) | async-done | bytes 134217744 | tf_op jit(solution)/shard_map/all_gather | solution.py:18
  384.2 4.8 slice.287
  389.0 156.3 %copy.3 = bf16[8192,32,256]{0,2,1:T(8,128)(2,1)} copy(bf16[8192,32,256]{2,0,1:T(8,128)(2,1)} %bitcast.1) | data formatting | bytes 268435456 | tf_op jit(solution)/shard_map/transpose | solution.py:25
  545.3 6.4 copy.4
  559.6 3.4 fusion.178
  563.1 3.8 fusion.230
  566.9 4.0 fusion.311
  570.8 4.4 fusion.322
  578.6 3.5 fusion.308
  582.0 3.7 fusion.303
  585.7 3.8 fusion.314
  589.5 4.0 fusion.298
  593.5 4.2 fusion.293
  597.8 4.7 fusion.288
  602.5 4.6 fusion.283
  607.1 4.7 fusion.278
  611.8 4.9 fusion.225
  616.7 5.1 fusion.220
  621.8 5.3 fusion.273
  627.1 5.6 fusion.268
  632.7 5.6 fusion.263
  638.3 5.8 fusion.258
  644.1 6.0 fusion.253
  650.1 6.1 fusion.248
  656.2 6.5 fusion.243
  662.7 6.5 fusion.238
  669.2 6.7 fusion.233
  675.9 6.8 fusion.340
  682.7 7.3 fusion.335
  690.0 11.7 %fusion.330 = bf16[8192,1024]{1,0:T(8,128)(2,1)} fusion(bf16[8192,1024]{1,0:T(8,128)(2,1)} %fusion.335, bf16[8192,1024]{1,0:T(8,128)(2,1)} %param.3, bf16[8192,8192]{0,1:T(8,128)(2,1)} %bitcast.2), kind=kOutput, calls=%fused_computation.141 | convolution fusion | flops 4026793984 | bytes 20185088 | tf_op jit(solution)/shard_map/dot_general | solution.py:32
  701.7 12.2 %fusion.325 = bf16[8192,1024]{1,0:T(8,128)(2,1)} fusion(bf16[8192,1024]{1,0:T(8,128)(2,1)} %fusion.330, bf16[8192,1024]{1,0:T(8,128)(2,1)} %param.3, bf16[8192,8192]{0,1:T(8,128)(2,1)} %bitcast.2), kind=kOutput, calls=%fused_computation.140 | convolution fusion | flops 4161011712 | bytes 20840448 | tf_op jit(solution)/shard_map/dot_general | solution.py:32
  713.9 9.0 %fusion.219 = bf16[8192,1024]{1,0:T(8,128)(2,1)} fusion(bf16[8192,1024]{1,0:T(8,128)(2,1)} %fusion.325, bf16[256,8192]{0,1:T(8,128)(2,1)S(1)} %bitcast.9, bf16[8192,1024]{1,0:T(8,128)(2,1)} %param.3), kind=kOutput, calls=%fused_computation.116 | convolution fusion | flops 4295229440 | bytes 21495808 | tf_op jit(solution)/shard_map/dot_general | solution.py:32
  (17 shorter events, 12.0 us)
Async XLA Ops:
  6.5 377.7 %all-gather.3.cloned.1.call-start = ((), (), s32[]{:S(2)}) async-start(), calls=%async_computation | async-start | bytes 138412032 | tf_op jit(solution)/shard_map/all_gather | solution.py:18
  551.7 23.5 %slice-start = ((s8[16777216]{0:T(1024)(128)(4,1)}), s8[4194304]{0:T(1024)(128)(4,1)S(1)}, s32[]{:S(2)}) async-start(s8[16777216]{0:T(1024)(128)(4,1)} %bitcast.7), calls=%async_computation.1 | async-start | bytes 8388608
  559.6 15.6 %slice-start.1 = ((s8[16777216]{0:T(1024)(128)(4,1)}), s8[4194304]{0:T(1024)(128)(4,1)S(1)}, s32[]{:S(2)}) async-start(s8[16777216]{0:T(1024)(128)(4,1)} %bitcast.7), calls=%async_computation.2 | async-start | bytes 8388608
  563.1 12.2 %slice-start.2 = ((s8[16777216]{0:T(1024)(128)(4,1)}), s8[4194304]{0:T(1024)(128)(4,1)S(1)}, s32[]{:S(2)}) async-start(s8[16777216]{0:T(1024)(128)(4,1)} %bitcast.7), calls=%async_computation.3 | async-start | bytes 8388608
  570.8 4.4 slice-start.3
  701.7 12.2 %copy-start = (bf16[256,32,256]{0,2,1:T(8,128)(2,1)S(1)}, bf16[256,32,256]{0,2,1:T(8,128)(2,1)}, u32[]{:S(2)}) copy-start(bf16[256,32,256]{0,2,1:T(8,128)(2,1)} %copy.4) | copy-start | bytes 12582916
Sparse Core Ops, SparseCore 0:
  9.4 374.7 all-gather.2
where the time goes:
time: 745 us; the launch traced here: 730 us
  waiting for transfers between devices  378 us (51%)
  matrix products  171 us (23%)
  local copies, waits for them, and re-layouts  168 us (23%)
  between operations  13.9 us (2%)
    all_gather x1, waiting for transfers between devices, local_product(): gathered = lax.all_gather(packed, 'col')  377 us
    dot_general x32, matrix products, local_product(): jnp.dot(strip, b_cols[:row_end], preferred_element_type=jnp.float32)  171 us
    transpose x1, local copies, waits for them, and re-layouts, local_product(): jnp.transpose(panel_band, (1, 0, 2)).reshape(band_rows, super_width)  156 us
  transfers between devices with their start and end apart: 1, of which 1 were waited for; matrix products, arithmetic and copies ran while one was open for 0% of the time, Pallas kernels for 0%

commit v1 on v0

v1 whole, which is shorter than its diff:
```python
import functools
import math

import jax
import jax.numpy as jnp
from jax import lax
from jax.experimental import pallas as pl
from jax.experimental.pallas import tpu as pltpu
from jax.sharding import PartitionSpec as P

MESH = pl.DeviceIdType.MESH
OFFS = (0, -1, 1, 2)


def kernel(side, l_ref, b_ref, y_ref, g_ref, b_vm, acc, l_vm, st_x, st_y, out_st,
           own_sem, par_sem, send_sem, loc_sem, fold_sem, load_sem, stx_sem, sty_sem, out_sem):
    rows, blk = l_ref.shape
    cols = b_ref.shape[1]
    per_row = 2 * side
    n_part = per_row
    n_full = (side - 1) * per_row // 2
    n_slot = n_part + n_full
    n_iter = n_slot // 2
    me = lax.axis_index("col")
    k = lax.rem(me, 2)
    x = lax.rem(me // 2, side)
    y = me // (2 * side)

    def wrap(v):
        return lax.rem(v + 2 * side, side)

    def dev(yy, xx, kk):
        return {"col": (yy * side + xx) * 2 + kk}

    def where3(c, a, b):
        return jnp.where(c, a, b)

    def strip_of(r, yy):
        f = r - n_part
        full_strip = where3(yy < 2, 20 + f, where3(yy == 2, where3(f < 8, 24 + f, 8 + f), 8 + f))
        full_grp = where3(yy == 0, 0, where3(yy == 1, 1, where3(yy == 2, where3(f < 8, 2, 1), 0)))
        part = r < n_part
        return where3(part, per_row * yy + per_row - 1 - r, full_strip), where3(part, yy, full_grp)

    def exists(r, xx, kk):
        return (r >= n_part) | (2 * xx + kk <= per_row - 1 - r)

    def chunk(r, yy, xx, kk):
        return g_ref.at[r, yy, :, pl.ds(pl.multiple_of((2 * xx + kk) * blk, blk), blk)]

    def pos(first_x, da, db):
        return (wrap(y + db), wrap(x + da)) if first_x else (wrap(y + da), wrap(x + db))

    def plus_dir(is_x, t, src):
        alt = lax.rem(t + src, 2) == 0
        if is_x:
            return alt
        return jnp.where(src == 1, lax.rem(t, 3) != 0, alt)

    def rcopy(r, yy, xx, dst, s, to_partner=False):
        c = chunk(r, yy, xx, k)
        rs = par_sem if to_partner else own_sem
        return pltpu.make_async_remote_copy(
            src_ref=c, dst_ref=c, send_sem=send_sem.at[r, s], recv_sem=rs.at[r, yy * side + xx],
            device_id=dst, device_id_type=MESH)

    def wait_own(r, yy, xx):
        rcopy(r, yy, xx, dev(y, x, k), 0).wait_recv()

    def wait_par(r, yy, xx):
        c = chunk(r, yy, xx, 1 - k)
        pltpu.make_async_copy(c, c, par_sem.at[r, yy * side + xx]).wait()

    def wait_sent(r, s, n):
        c = g_ref.at[0, 0, :, pl.ds(0, n * blk)]
        pltpu.make_async_copy(c, c, send_sem.at[r, s]).wait()

    def neighbour(first_x, first_axis, d):
        on_x = first_x == first_axis
        return dev(y, wrap(x + d), k) if on_x else dev(wrap(y + d), x, k)

    partner = dev(y, x, 1 - k)

    def own_local(r):
        return (r < n_part) | (y < 2) | ((y == 2) & (r < n_part + 8))

    def local_copy(r):
        strip, _ = strip_of(r, y)
        return pltpu.make_async_copy(
            l_vm.at[pl.ds(pl.multiple_of(strip * blk, blk), blk), :], chunk(r, y, x, k), loc_sem.at[r])

    def inject(t):
        for first_x in (True, False):
            r = 2 * t + (0 if first_x else 1)

            @pl.when(exists(r, x, k))
            def _():
                @pl.when(own_local(r))
                def _():
                    local_copy(r).wait()

                @pl.when(jnp.logical_not(own_local(r)))
                def _():
                    wait_own(r, y, x)

                for d in (1, -1):
                    rcopy(r, y, x, neighbour(first_x, True, d), 0).start()
                for d in (1, -1):
                    rcopy(r, y, x, neighbour(first_x, False, d), 0).start()
                rcopy(r, y, x, partner, 0, True).start()

    def first_step(t, i):
        for first_x in (True, False):
            r = 2 * t + (0 if first_x else 1)
            yy, xx = pos(first_x, OFFS[i], 0)

            @pl.when(exists(r, xx, k))
            def _():
                wait_own(r, yy, xx)
                if i < 3:
                    src = xx if first_x else yy
                    plus = plus_dir(first_x, t, src)
                    fwd = plus if i == 1 else jnp.logical_not(plus)

                    @pl.when(fwd)
                    def _():
                        rcopy(r, yy, xx, neighbour(first_x, True, 1 if i == 1 else -1), 3 + i).start()
                for d in (1, -1):
                    rcopy(r, yy, xx, neighbour(first_x, False, d), i).start()
                rcopy(r, yy, xx, partner, i, True).start()

    def second_step(t, i):
        for first_x in (True, False):
            r = 2 * t + (0 if first_x else 1)
            for a in range(4):
                yy, xx = pos(first_x, OFFS[a], OFFS[i])

                @pl.when(exists(r, xx, k))
                def _():
                    wait_own(r, yy, xx)
                    if i < 3:
                        src = yy if first_x else xx
                        plus = plus_dir(not first_x, t, src)
                        fwd = plus if i == 1 else jnp.logical_not(plus)

                        @pl.when(fwd)
                        def _():
                            rcopy(r, yy, xx, neighbour(first_x, False, 1 if i == 1 else -1),
                                  6 + 12 + 4 * (i - 1) + a).start()
                    rcopy(r, yy, xx, partner, 6 + 4 * (i - 1) + a, True).start()

    def drain_first(t):
        for first_x in (True, False):
            r = 2 * t + (0 if first_x else 1)

            @pl.when(exists(r, x, k))
            def _():
                wait_sent(r, 0, 5)
            for i in (1, 2, 3):
                yy, xx = pos(first_x, OFFS[i], 0)

                @pl.when(exists(r, xx, k))
                def _():
                    wait_sent(r, i, 3)
                    if i < 3:
                        plus = plus_dir(first_x, t, xx if first_x else yy)

                        @pl.when(plus if i == 1 else jnp.logical_not(plus))
                        def _():
                            wait_sent(r, 3 + i, 1)

    def drain_second(t):
        for first_x in (True, False):
            r = 2 * t + (0 if first_x else 1)
            for i in (1, 2, 3):
                for a in range(4):
                    yy, xx = pos(first_x, OFFS[a], OFFS[i])

                    @pl.when(exists(r, xx, k))
                    def _():
                        wait_sent(r, 6 + 4 * (i - 1) + a, 1)
                        if i < 3:
                            plus = plus_dir(not first_x, t, yy if first_x else xx)

                            @pl.when(plus if i == 1 else jnp.logical_not(plus))
                            def _():
                                wait_sent(r, 6 + 12 + 4 * (i - 1) + a, 1)

    def fold_copy(f):
        r = n_part + f
        strip = 8 + f
        return pltpu.make_async_remote_copy(
            src_ref=l_vm.at[pl.ds(pl.multiple_of(strip * blk, blk), blk), :],
            dst_ref=chunk(r, 3 - y, x, k), send_sem=fold_sem.at[f],
            recv_sem=own_sem.at[r, (3 - y) * side + x],
            device_id=dev(3 - y, x, k), device_id_type=MESH)

    def fold_cond(f):
        return (y == 0) | ((y == 1) & (f >= 8))

    def stage_x(t, i, buf):
        return pltpu.make_async_copy(g_ref.at[2 * t, wrap(y + OFFS[i])], st_x.at[buf], stx_sem.at[buf])

    def stage_y(t, i, buf, yy):
        xx = wrap(x + OFFS[i])
        return pltpu.make_async_copy(
            g_ref.at[2 * t + 1, yy, :, pl.ds(pl.multiple_of(xx * 2 * blk, 2 * blk), 2 * blk)],
            st_y.at[buf, yy], sty_sem.at[buf])

    def push(t, i, buf):
        for first_x in (True, False):
            r = 2 * t + (0 if first_x else 1)
            for a in range(4):
                yy, xx = pos(first_x, OFFS[a], OFFS[i])

                @pl.when(exists(r, xx, 1 - k))
                def _():
                    wait_par(r, yy, xx)
            if first_x:
                stage_x(t, i, buf).start()
            else:
                for yy in range(side):
                    stage_y(t, i, buf, yy).start()

    def add_dot(lhs, row0, n_rows, strip):
        row0 = pl.multiple_of(row0, 2 * blk)
        arow = pl.multiple_of(strip * blk, blk)
        wn = min(256, cols)
        for n in range(cols // wn):
            acc[pl.ds(arow, blk), n * wn:(n + 1) * wn] += jnp.dot(
                lhs, b_vm[pl.ds(row0, n_rows), n * wn:(n + 1) * wn], preferred_element_type=jnp.float32)

    def compute(t, i, buf):
        r = 2 * t
        stage_x(t, i, buf).wait()
        yy = wrap(y + OFFS[i])

        @pl.when(r < n_part)
        def _():
            for m in range(1, per_row):
                @pl.when(m > per_row - 1 - r)
                def _():
                    st_x[buf, :, m * blk:(m + 1) * blk] = jnp.zeros((blk, blk), st_x.dtype)
        strip, grp = strip_of(r, yy)
        add_dot(st_x[buf], grp * (per_row * blk), per_row * blk, strip)

        r = 2 * t + 1
        c = st_y.at[buf]
        pltpu.make_async_copy(c, c, sty_sem.at[buf]).wait()
        xx = wrap(x + OFFS[i])

        @pl.when(r < n_part)
        def _():
            for kk in range(2):
                @pl.when(2 * xx + kk > per_row - 1 - r)
                def _():
                    st_y[buf, :, :, kk * blk:(kk + 1) * blk] = jnp.zeros((side, blk, blk), st_y.dtype)
        for yy in range(side):
            strip, grp = strip_of(r, yy)
            add_dot(st_y[buf, yy], grp * (per_row * blk) + xx * (2 * blk), 2 * blk, strip)

    def out_copy(strip, buf):
        return pltpu.make_async_copy(
            out_st.at[buf], y_ref.at[pl.ds(pl.multiple_of(strip * blk, blk), blk), :], out_sem.at[buf])

    def out_strips(t):
        for s in range(2):
            r = 2 * t + s
            f = r - n_part
            yield 2 * s, where3(r < n_part, per_row - 1 - r, 20 + f), None
            yield 2 * s + 1, 8 + f, r >= n_part

    def emit(t):
        for buf, strip, cond in out_strips(t):
            def go():
                out_st[buf] = acc[pl.ds(pl.multiple_of(strip * blk, blk), blk), :].astype(out_st.dtype)
                out_copy(strip, buf).start()
            if cond is None:
                go()
            else:
                pl.when(cond)(go)

    def emit_wait(t):
        for buf, strip, cond in out_strips(t):
            def go():
                out_copy(strip, buf).wait()
            if cond is None:
                go()
            else:
                pl.when(cond)(go)

    l_load = pltpu.make_async_copy(l_ref, l_vm, load_sem.at[0])
    l_load.start()
    b_load = pltpu.make_async_copy(b_ref, b_vm, load_sem.at[1])
    b_load.start()
    barrier = pltpu.get_barrier_semaphore()
    for d in (dev(y, wrap(x + 1), k), dev(y, wrap(x - 1), k), dev(wrap(y + 1), x, k), dev(wrap(y - 1), x, k), partner):
        pl.semaphore_signal(barrier, inc=1, device_id=d, device_id_type=MESH)
    l_load.wait()

    def start_local(r, _):
        @pl.when(exists(r, x, k) & own_local(r))
        def _():
            local_copy(r).start()
        return 0
    lax.fori_loop(0, n_slot, start_local, 0)
    pl.semaphore_wait(barrier, 5)
    inject(0)
    inject(1)

    def zero(i, _):
        acc[pl.ds(pl.multiple_of(i * blk, blk), blk), :] = jnp.zeros((blk, cols), acc.dtype)
        return 0
    lax.fori_loop(0, rows // blk, zero, 0)
    for i in (1, 2, 3):
        first_step(0, i)
    push(0, 0, 0)
    b_load.wait()

    def body(t, _):
        more1 = t + 1 < n_iter

        @pl.when(t + 2 < n_iter)
        def _():
            inject(t + 2)

        @pl.when(t < n_full // 2)
        def _():
            for s in range(2):
                @pl.when(fold_cond(2 * t + s))
                def _():
                    fold_copy(2 * t + s).start()

        @pl.when(more1)
        def _():
            first_step(t + 1, 1)
            first_step(t + 1, 2)
        second_step(t, 1)
        push(t, 1, 1)

        @pl.when(t == 0)
        def _():
            compute(0, 0, 0)

        @pl.when(t > 0)
        def _():
            compute(t - 1, 3, 0)

            @pl.when(t > 1)
            def _():
                emit_wait(t - 2)
            emit(t - 1)

        @pl.when(more1)
        def _():
            first_step(t + 1, 3)
            push(t + 1, 0, 0)
        compute(t, 1, 1)
        second_step(t, 2)
        push(t, 2, 1)

        @pl.when(more1)
        def _():
            compute(t + 1, 0, 0)
        second_step(t, 3)
        push(t, 3, 0)
        compute(t, 2, 1)
        drain_first(t)

        @pl.when(t > 0)
        def _():
            drain_second(t - 1)
        return 0
    lax.fori_loop(0, n_iter, body, 0)

    compute(n_iter - 1, 3, 0)
    emit_wait(n_iter - 2)
    emit(n_iter - 1)

    def fold_drain(f, _):
        @pl.when(fold_cond(f))
        def _():
            fold_copy(f).wait_send()
        return 0
    lax.fori_loop(0, n_full, fold_drain, 0)
    drain_second(n_iter - 1)
    emit_wait(n_iter - 1)


def solution(mesh):
    group_size = mesh.shape["col"]
    side = math.isqrt(group_size // 2)

    def local_product(l_cols, b_cols):
        rows, blk = l_cols.shape
        cols = b_cols.shape[1]
        per_row = 2 * side
        n_slot = per_row + (side - 1) * per_row // 2
        dma = pltpu.SemaphoreType.DMA
        product, _ = pl.pallas_call(
            functools.partial(kernel, side),
            out_shape=(
                jax.ShapeDtypeStruct((rows, cols), jnp.bfloat16),
                jax.ShapeDtypeStruct((n_slot, side, blk, per_row * blk), jnp.bfloat16),
            ),
            in_specs=[pl.BlockSpec(memory_space=pl.ANY)] * 2,
            out_specs=(pl.BlockSpec(memory_space=pl.ANY),) * 2,
            scratch_shapes=[
                pltpu.VMEM((rows, cols), jnp.bfloat16),
                pltpu.VMEM((rows, cols), jnp.float32),
                pltpu.VMEM((rows, blk), jnp.bfloat16),
                pltpu.VMEM((2, blk, per_row * blk), jnp.bfloat16),
                pltpu.VMEM((2, side, blk, 2 * blk), jnp.bfloat16),
                pltpu.VMEM((4, blk, cols), jnp.bfloat16),
                dma((n_slot, side * side)),
                dma((n_slot, side * side)),
                dma((n_slot, 26)),
                dma((n_slot,)),
                dma((n_slot - per_row,)),
                dma((2,)),
                dma((2,)),
                dma((2,)),
                dma((4,)),
            ],
            compiler_params=pltpu.CompilerParams(
                collective_id=0, has_side_effects=True, vmem_limit_bytes=67043328),
            cost_estimate=pl.CostEstimate(flops=rows * rows * cols, bytes_accessed=4 * rows * cols, transcendentals=0),
        )(l_cols, b_cols)
        return product

    return jax.shard_map(local_product, mesh=mesh, in_specs=(P("batch", "col"), P("batch", "col")), out_specs=P("batch", "col"), check_vma=False)
```

time: 745 us -> 390 us (0.52); the launches traced: 730 us -> 389 us
  waiting for transfers between devices: 378 us -> 0 us
  Pallas kernels: 0 us -> 375 us
  matrix products: 171 us -> 0 us
  local copies, waits for them, and re-layouts: 168 us -> 13.9 us
  between operations: 13.9 us -> 0.01 us
    all_gather x1 -> x0, waiting for transfers between devices: 377 us -> none  [local_product(): gathered = lax.all_gather(packed, 'col')]
    pallas_call x0 -> x1, Pallas kernels: none -> 375 us  [local_product(): pl.pallas_call(functools.partial(kernel, side), out_shape=(jax.ShapeDtype...]
    dot_general x32 -> x0, matrix products: 171 us -> none  [local_product(): jnp.dot(strip, b_cols[:row_end], preferred_element_type=jnp.float32)]
    transpose x1 -> x0, local copies, waits for them, and re-layouts: 156 us -> none  [local_product(): jnp.transpose(panel_band, (1, 0, 2)).reshape(band_rows, super_width)]
    unnamed x10 -> x1, local copies, waits for them, and re-layouts: 0.02 us -> 13.9 us
    slice x2 -> x0, local copies, waits for them, and re-layouts: 11.2 us -> none  [local_product(): strip = natural[row_idx * BLOCK_SIZE:row_end, :row_end]]
  transfers between devices with their start and end apart: 1 -> 0, of which waited for: 1 -> 0; matrix products, arithmetic and copies ran while one was open for 0% -> 0% of each run, Pallas kernels for 0% -> 0%
where the time goes in v1:
time: 390 us; the launch traced here: 389 us
  Pallas kernels  375 us (96%)
  local copies, waits for them, and re-layouts  13.9 us (4%)
    pallas_call x1, Pallas kernels, local_product(): pl.pallas_call(functools.partial(kernel, side), out_shape=(jax.ShapeDtype...  375 us
    unnamed x1, local copies, waits for them, and re-layouts  13.9 us

profile of v1, /device:TPU:97, one launch (start us, length us, event | category | flops | bytes accessed | tf_op | source)
XLA Modules:
  0.0 389.4 jit_solution(3407071053610451725)
XLA Ops:
  0.0 375.5 %shard_map.28 = (bf16[8192,1024]{1,0:T(8,128)(2,1)}, bf16[20,4,256,2048]{3,2,1,0:T(8,128)(2,1)}) custom-call(bf16[8192,256]{1,0:T(8,128)(2,1)} %l_ref.1, bf16[8192,1024]{1,0:T(8,128)(2,1)} %b_ref.1), custom_call_target="tpu_custom_call" | custom-call | flops 68719476736 | bytes 33554432 | tf_op jit(solution)/shard_map/pallas_call | solution.py:400
  375.5 13.9 %copy.4 = bf16[8192,1024]{1,0:T(8,128)(2,1)} copy(bf16[8192,1024]{1,0:T(8,128)(2,1)} %get-tuple-element.6) | data formatting | bytes 33554432

commit v2 on v0

v2 whole, which is shorter than its diff:
```python
import functools
import math

import jax
import jax.numpy as jnp
from jax import lax
from jax.experimental import pallas as pl
from jax.experimental.pallas import tpu as pltpu
from jax.sharding import PartitionSpec as P

MESH = pl.DeviceIdType.MESH
OFFS = (0, -1, 1, 2)
DIAG = 6
FULL = 12
SLOTS = DIAG + FULL
PAIRS = SLOTS // 2
FULL_PAIR = DIAG // 2
DIAG_WORK = {2: (7, 6, 0), 3: (5, 1), 4: (4,), 5: (3, 2)}
DIAG_ORDER = sum(DIAG_WORK.values(), ())


def diag_place(p, m):
    k, h = m % 2, m // 2
    main = {0: {6: 1, 7: 2, 4: 3, 5: 4, 3: 5}, 1: {7: 2, 6: 3, 5: 4, 4: 5}}[k]
    alt = {0: {0: 3, 1: 4, 2: 5}, 1: {2: 3, 1: 4, 3: 5}}[k]
    if p in main:
        return main[p], h
    return alt[p], 3 - h


def kernel(side, l_ref, b_ref, y_ref, g_ref, b_vm, acc, l_vm, st_x, st_y, st_d, out_st,
           own_sem, far_sem, par_sem, send_sem, loc_sem, fold_sem, xfold_sem, load_sem,
           stx_sem, sty_sem, std_sem, out_sem, outd_sem):
    rows, blk = l_ref.shape
    cols = b_ref.shape[1]
    per_row = 2 * side
    wide = per_row * blk
    me = lax.axis_index("col")
    k = lax.rem(me, 2)
    x = lax.rem(me // 2, side)
    y = me // (2 * side)
    where = jnp.where

    def wrap(v):
        return lax.rem(v + 2 * side, side)

    def dev(yy, xx, kk):
        return {"col": (yy * side + xx) * 2 + kk}

    partner = dev(y, x, 1 - k)

    def full_strip(f, yy):
        strip = where(yy < 2, 20 + f, where((yy == 2) & (f < 8), 24 + f, 8 + f))
        grp = where(yy == 1, 1, where(yy == 2, where(f < 8, 2, 1), 0))
        return strip, grp

    def diag_main(r):
        return x < where(r <= 2, 4, where(r <= 4, 3, 2))

    def diag_strip(r):
        main = where(r == 1, 6, where(r == 2, 7, where(r == 3, 4 + 2 * k, where(r == 4, 5, 3 + k))))
        alt = where(r == 3, 2 * k, where(r == 4, 1, 2 + k))
        return main, alt

    def exists(r, kk):
        return (r >= 2) | ((r == 1) & (kk == 0))

    def chunk(r, yy, xx, kk):
        return g_ref.at[r, yy, kk, xx]

    def pos(first_x, da, db):
        return (wrap(y + db), wrap(x + da)) if first_x else (wrap(y + da), wrap(x + db))

    def plus_dir(is_x, t, src):
        alt = lax.rem(t + src, 2) == 0
        if is_x:
            return alt
        return where(src == 1, lax.rem(t, 3) != 0, alt)

    def neighbour(first_x, first_axis, d):
        on_x = first_x == first_axis
        return dev(y, wrap(x + d), k) if on_x else dev(wrap(y + d), x, k)

    def slots(t):
        return ((True, 2 * t), (False, 2 * t + 1))

    def rcopy(r, yy, xx, dst, s, rsem):
        c = chunk(r, yy, xx, k)
        return pltpu.make_async_remote_copy(
            src_ref=c, dst_ref=c, send_sem=send_sem.at[r, s], recv_sem=rsem,
            device_id=dst, device_id_type=MESH)

    def osem(r, yy, xx):
        return own_sem.at[r, yy * side + xx]

    def wait_n(sem, n):
        c = g_ref.at[pl.ds(0, n), 0, 0, 0]
        pltpu.make_async_copy(c, c, sem).wait()

    def group(r, first_x, i, kk):
        if first_x:
            return g_ref.at[r, wrap(y + OFFS[i]), kk]
        return g_ref.at[r, :, kk, wrap(x + OFFS[i])]

    def to_partner(first_x, r, i):
        c = group(r, first_x, i, k)
        pltpu.make_async_remote_copy(
            src_ref=c, dst_ref=c, send_sem=send_sem.at[r, 5], recv_sem=par_sem.at[r, i],
            device_id=partner, device_id_type=MESH).start()

    def own_local(r):
        return where(r < DIAG, diag_main(r), (y < 2) | ((y == 2) & (r < DIAG + 8)))

    def l_strip(strip):
        return l_vm.at[pl.ds(pl.multiple_of(strip * blk, blk), blk), :]

    def local_copy(r):
        strip = where(r < DIAG, per_row * y + diag_strip(r)[0], full_strip(r - DIAG, y)[0])
        return pltpu.make_async_copy(l_strip(strip), chunk(r, y, x, k), loc_sem.at[r])

    def inject(t):
        for first_x, r in slots(t):
            @pl.when(exists(r, k))
            def _():
                @pl.when(own_local(r))
                def _():
                    local_copy(r).wait()

                @pl.when(jnp.logical_not(own_local(r)))
                def _():
                    wait_n(osem(r, y, x), 1)

                for first_axis in (True, False):
                    for d in (1, -1):
                        rcopy(r, y, x, neighbour(first_x, first_axis, d), 0, osem(r, y, x)).start()

    def first_step(t, i):
        for first_x, r in slots(t):
            yy, xx = pos(first_x, OFFS[i], 0)

            @pl.when(exists(r, k))
            def _():
                wait_n(osem(r, yy, xx), 1)
                if i < 3:
                    plus = plus_dir(first_x, t, xx if first_x else yy)

                    @pl.when(plus if i == 1 else jnp.logical_not(plus))
                    def _():
                        rcopy(r, yy, xx, neighbour(first_x, True, 1 if i == 1 else -1), i, osem(r, yy, xx)).start()
                for d in (1, -1):
                    rcopy(r, yy, xx, neighbour(first_x, False, d), 0, osem(r, yy, xx)).start()
                if i == 3:
                    to_partner(first_x, r, 0)

    def second_step(t):
        for i in (1, 2):
            for first_x, r in slots(t):
                @pl.when(exists(r, k))
                def _():
                    p0, q0 = pos(first_x, 0, OFFS[i])
                    plus = plus_dir(not first_x, t, p0 if first_x else q0)
                    fwd = plus if i == 1 else jnp.logical_not(plus)
                    for a in range(4):
                        yy, xx = pos(first_x, OFFS[a], OFFS[i])
                        wait_n(osem(r, yy, xx), 1)

                        @pl.when(fwd)
                        def _():
                            rcopy(r, yy, xx, neighbour(first_x, False, 1 if i == 1 else -1), 2 + i,
                                  far_sem.at[r]).start()
                    to_partner(first_x, r, i)

    def far_step(t):
        for first_x, r in slots(t):
            @pl.when(exists(r, k))
            def _():
                wait_n(far_sem.at[r], 4)
                to_partner(first_x, r, 3)

    def drain(t):
        for first_x, r in slots(t):
            @pl.when(exists(r, k))
            def _():
                wait_n(send_sem.at[r, 0], 10)
                for i in (1, 2):
                    yy, xx = pos(first_x, OFFS[i], 0)
                    plus = plus_dir(first_x, t, xx if first_x else yy)

                    @pl.when(plus if i == 1 else jnp.logical_not(plus))
                    def _():
                        wait_n(send_sem.at[r, i], 1)
                    yy, xx = pos(first_x, 0, OFFS[i])
                    plus = plus_dir(not first_x, t, yy if first_x else xx)

                    @pl.when(plus if i == 1 else jnp.logical_not(plus))
                    def _():
                        wait_n(send_sem.at[r, 2 + i], 4)
                wait_n(send_sem.at[r, 5], 4 * side)

    def fold_copy(f):
        r = DIAG + f
        return pltpu.make_async_remote_copy(
            src_ref=l_strip(8 + f), dst_ref=chunk(r, 3 - y, x, k), send_sem=fold_sem.at[f],
            recv_sem=osem(r, 3 - y, x), device_id=dev(3 - y, x, k), device_id_type=MESH)

    def fold_cond(f):
        return (y == 0) | ((y == 1) & (f >= 8))

    def xfold(r):
        return pltpu.make_async_remote_copy(
            src_ref=l_strip(per_row * y + diag_strip(r)[1]), dst_ref=chunk(r, y, 3 - x, k),
            send_sem=xfold_sem.at[r], recv_sem=osem(r, y, 3 - x), device_id=dev(y, 3 - x, k), device_id_type=MESH)

    def xfold_cond(r):
        return (x == 0) | ((x == 1) & (r == 5))

    def stage(t, i, buf):
        yy = wrap(y + OFFS[i])
        xx = wrap(x + OFFS[i])
        for kk in range(2):
            for j in range(side):
                pltpu.make_async_copy(
                    g_ref.at[2 * t, yy, kk, j],
                    st_x.at[buf, :, (2 * j + kk) * blk:(2 * j + kk + 1) * blk], stx_sem.at[buf]).start()
                pltpu.make_async_copy(
                    g_ref.at[2 * t + 1, j, kk, xx],
                    st_y.at[buf, j, :, kk * blk:(kk + 1) * blk], sty_sem.at[buf]).start()

    def par_wait(t, i):
        for first_x, r in slots(t):
            @pl.when(exists(r, 1 - k))
            def _():
                wait_n(par_sem.at[r, i], 4)

    def push(t, i, buf):
        par_wait(t, i)

        @pl.when(t >= FULL_PAIR)
        def _():
            stage(t, i, buf)

    def add_dot(lhs, row0, n_rows, strip):
        row0 = pl.multiple_of(row0, 2 * blk)
        arow = pl.multiple_of(strip * blk, blk)
        wn = min(256, cols)
        for n in range(cols // wn):
            acc[pl.ds(arow, blk), n * wn:(n + 1) * wn] += jnp.dot(
                lhs, b_vm[pl.ds(row0, n_rows), n * wn:(n + 1) * wn], preferred_element_type=jnp.float32)

    def compute(t, i, buf):
        c = st_x.at[buf]
        pltpu.make_async_copy(c, c, stx_sem.at[buf]).wait()
        strip, grp = full_strip(2 * t - DIAG, wrap(y + OFFS[i]))
        add_dot(st_x[buf], grp * wide, wide, strip)

        c = st_y.at[buf]
        pltpu.make_async_copy(c, c, sty_sem.at[buf]).wait()
        xx = wrap(x + OFFS[i])
        for yy in range(side):
            strip, grp = full_strip(2 * t + 1 - DIAG, yy)
            add_dot(st_y[buf, yy], grp * wide + xx * (2 * blk), 2 * blk, strip)

    def diag_stage(p, yy, buf):
        for m in range(p + 1):
            r, xx = diag_place(p, m)
            pltpu.make_async_copy(
                g_ref.at[r, yy, m % 2, xx], st_d.at[buf, :, m * blk:(m + 1) * blk], std_sem.at[buf]).start()

    def diag_compute(p):
        n = (p + 1) * blk
        diag_stage(p, 0, 0)

        def one(yy, _):
            buf = lax.rem(yy, 2)

            @pl.when(yy + 1 < side)
            def _():
                diag_stage(p, yy + 1, 1 - buf)
            c = st_d.at[buf, :, pl.ds(0, n)]
            pltpu.make_async_copy(c, c, std_sem.at[buf]).wait()
            add_dot(st_d[buf, :, :n], yy * wide, n, per_row * yy + p)
            return 0
        lax.fori_loop(0, side, one, 0)

    def out_copy(strip, buf, sem):
        return pltpu.make_async_copy(
            out_st.at[buf], y_ref.at[pl.ds(pl.multiple_of(strip * blk, blk), blk), :], sem)

    def put(strip, buf, sem):
        out_st[buf] = acc[pl.ds(pl.multiple_of(strip * blk, blk), blk), :].astype(out_st.dtype)
        out_copy(strip, buf, sem).start()

    def out_strips(t):
        f = 2 * t - DIAG
        return ((0, 20 + f), (1, 8 + f), (2, 21 + f), (3, 9 + f))

    def emit(t):
        for buf, strip in out_strips(t):
            put(strip, buf, out_sem.at[buf])

    def emit_wait(t):
        for buf, strip in out_strips(t):
            out_copy(strip, buf, out_sem.at[buf]).wait()

    l_load = pltpu.make_async_copy(l_ref, l_vm, load_sem.at[0])
    l_load.start()
    b_load = pltpu.make_async_copy(b_ref, b_vm, load_sem.at[1])
    b_load.start()
    barrier = pltpu.get_barrier_semaphore()
    for d in (dev(y, wrap(x + 1), k), dev(y, wrap(x - 1), k), dev(wrap(y + 1), x, k), dev(wrap(y - 1), x, k), partner):
        pl.semaphore_signal(barrier, inc=1, device_id=d, device_id_type=MESH)
    l_load.wait()

    def start_local(r, _):
        @pl.when(exists(r, k) & own_local(r))
        def _():
            local_copy(r).start()
        return 0
    lax.fori_loop(0, SLOTS, start_local, 0)
    pl.semaphore_wait(barrier, 5)
    for r in (3, 4, 5):
        @pl.when(xfold_cond(r))
        def _():
            xfold(r).start()
    inject(0)
    inject(1)

    def zero(i, _):
        acc[pl.ds(pl.multiple_of(i * blk, blk), blk), :] = jnp.zeros((blk, cols), acc.dtype)
        return 0
    lax.fori_loop(0, rows // blk, zero, 0)
    for r in (3, 4, 5):
        @pl.when(xfold_cond(r))
        def _():
            xfold(r).wait_send()
    b_load.wait()

    def body(n, _):
        t = n - 1
        now = (t >= 0) & (t < PAIRS)
        now_full = (t >= FULL_PAIR) & (t < PAIRS)
        before = t >= 1
        before_full = t > FULL_PAIR
        after = t + 1 < PAIRS

        @pl.when((t >= 0) & (t + 2 < PAIRS))
        def _():
            inject(t + 2)

        @pl.when(t + 1 < FULL // 2)
        def _():
            for s in range(2):
                f = 2 * (t + 1) + s

                @pl.when(fold_cond(f))
                def _():
                    fold_copy(f).start()

        @pl.when(after)
        def _():
            first_step(t + 1, 1)
            first_step(t + 1, 2)

        @pl.when(now)
        def _():
            second_step(t)

        @pl.when(before)
        def _():
            far_step(t - 1)

        @pl.when(now)
        def _():
            push(t, 1, 1)

        @pl.when(now_full)
        def _():
            compute(t, 0, 0)

        @pl.when(now)
        def _():
            push(t, 2, 0)

        @pl.when(now_full)
        def _():
            compute(t, 1, 1)

        @pl.when(after)
        def _():
            first_step(t + 1, 3)

        @pl.when(before)
        def _():
            push(t - 1, 3, 1)

        @pl.when(now_full)
        def _():
            compute(t, 2, 0)

        @pl.when(after)
        def _():
            push(t + 1, 0, 0)

        @pl.when(before_full)
        def _():
            compute(t - 1, 3, 1)
        for tt, ps in DIAG_WORK.items():
            @pl.when(t == tt)
            def _():
                for p in ps:
                    diag_compute(p)
                    n_th = DIAG_ORDER.index(p)
                    if n_th:
                        out_copy(DIAG_ORDER[n_th - 1], 4, outd_sem.at[0]).wait()
                    put(p, 4, outd_sem.at[0])

        @pl.when(before_full)
        def _():
            @pl.when(t > FULL_PAIR + 1)
            def _():
                emit_wait(t - 2)
            emit(t - 1)

        @pl.when(before)
        def _():
            drain(t - 1)
        return 0
    lax.fori_loop(0, PAIRS + 2, body, 0)

    def fold_drain(f, _):
        @pl.when(fold_cond(f))
        def _():
            fold_copy(f).wait_send()
        return 0
    lax.fori_loop(0, FULL, fold_drain, 0)
    emit_wait(PAIRS - 1)
    out_copy(DIAG_ORDER[-1], 4, outd_sem.at[0]).wait()


def solution(mesh):
    group_size = mesh.shape["col"]
    side = math.isqrt(group_size // 2)

    def local_product(l_cols, b_cols):
        rows, blk = l_cols.shape
        cols = b_cols.shape[1]
        per_row = 2 * side
        dma = pltpu.SemaphoreType.DMA
        product, _ = pl.pallas_call(
            functools.partial(kernel, side),
            out_shape=(
                jax.ShapeDtypeStruct((rows, cols), jnp.bfloat16),
                jax.ShapeDtypeStruct((SLOTS, side, 2, side, blk, blk), jnp.bfloat16),
            ),
            in_specs=[pl.BlockSpec(memory_space=pl.ANY)] * 2,
            out_specs=(pl.BlockSpec(memory_space=pl.ANY),) * 2,
            scratch_shapes=[
                pltpu.VMEM((rows, cols), jnp.bfloat16),
                pltpu.VMEM((rows, cols), jnp.float32),
                pltpu.VMEM((rows, blk), jnp.bfloat16),
                pltpu.VMEM((2, blk, per_row * blk), jnp.bfloat16),
                pltpu.VMEM((2, side, blk, 2 * blk), jnp.bfloat16),
                pltpu.VMEM((2, blk, per_row * blk), jnp.bfloat16),
                pltpu.VMEM((5, blk, cols), jnp.bfloat16),
                dma((SLOTS, side * side)),
                dma((SLOTS,)),
                dma((SLOTS, 4)),
                dma((SLOTS, 6)),
                dma((SLOTS,)),
                dma((FULL,)),
                dma((DIAG,)),
                dma((2,)),
                dma((2,)),
                dma((2,)),
                dma((2,)),
                dma((4,)),
                dma((1,)),
            ],
            compiler_params=pltpu.CompilerParams(
                collective_id=0, has_side_effects=True, vmem_limit_bytes=67043328),
            cost_estimate=pl.CostEstimate(flops=rows * rows * cols, bytes_accessed=4 * rows * cols, transcendentals=0),
        )(l_cols, b_cols)
        return product

    return jax.shard_map(local_product, mesh=mesh, in_specs=(P("batch", "col"), P("batch", "col")), out_specs=P("batch", "col"), check_vma=False)
```

time: 745 us -> 268 us (0.36); the launches traced: 730 us -> 267 us
  waiting for transfers between devices: 378 us -> 0 us
  Pallas kernels: 0 us -> 253 us
  matrix products: 171 us -> 0 us
  local copies, waits for them, and re-layouts: 168 us -> 13.9 us
  between operations: 13.9 us -> 0.01 us
    all_gather x1 -> x0, waiting for transfers between devices: 377 us -> none  [local_product(): gathered = lax.all_gather(packed, 'col')]
    pallas_call x0 -> x1, Pallas kernels: none -> 253 us  [local_product(): pl.pallas_call(functools.partial(kernel, side), out_shape=(jax.ShapeDtype...]
    dot_general x32 -> x0, matrix products: 171 us -> none  [local_product(): jnp.dot(strip, b_cols[:row_end], preferred_element_type=jnp.float32)]
    transpose x1 -> x0, local copies, waits for them, and re-layouts: 156 us -> none  [local_product(): jnp.transpose(panel_band, (1, 0, 2)).reshape(band_rows, super_width)]
    unnamed x10 -> x1, local copies, waits for them, and re-layouts: 0.02 us -> 13.9 us
    slice x2 -> x0, local copies, waits for them, and re-layouts: 11.2 us -> none  [local_product(): strip = natural[row_idx * BLOCK_SIZE:row_end, :row_end]]
  transfers between devices with their start and end apart: 1 -> 0, of which waited for: 1 -> 0; matrix products, arithmetic and copies ran while one was open for 0% -> 0% of each run, Pallas kernels for 0% -> 0%
where the time goes in v2:
time: 268 us; the launch traced here: 267 us
  Pallas kernels  253 us (94%)
  local copies, waits for them, and re-layouts  13.9 us (5%)
    pallas_call x1, Pallas kernels, local_product(): pl.pallas_call(functools.partial(kernel, side), out_shape=(jax.ShapeDtype...  253 us
    unnamed x1, local copies, waits for them, and re-layouts  13.9 us

profile of v2, /device:TPU:97, one launch (start us, length us, event | category | flops | bytes accessed | tf_op | source)
XLA Modules:
  0.0 267.0 jit_solution(5615668438699032291)
XLA Ops:
  0.0 253.1 %shard_map.28 = (bf16[8192,1024]{1,0:T(8,128)(2,1)}, bf16[18,4,2,4,256,256]{5,4,3,2,1,0:T(8,128)(2,1)}) custom-call(bf16[8192,256]{1,0:T(8,128)(2,1)} %l_ref.1, bf16[8192,1024]{1,0:T(8,128)(2,1)} %b_ref.1), custom_call_target="tpu_custom_call" | custom-call | flops 68719476736 | bytes 33554432 | tf_op jit(solution)/shard_map/pallas_call | solution.py:449
  253.1 13.9 %copy.4 = bf16[8192,1024]{1,0:T(8,128)(2,1)} copy(bf16[8192,1024]{1,0:T(8,128)(2,1)} %get-tuple-element.6) | data formatting | bytes 33554432

commit v3 on v2

--- a/solution.py
+++ b/solution.py
@@ -15,7 +15,7 @@
 SLOTS = DIAG + FULL
 PAIRS = SLOTS // 2
 FULL_PAIR = DIAG // 2
-DIAG_WORK = {2: (7, 6, 0), 3: (5, 1), 4: (4,), 5: (3, 2)}
+DIAG_WORK = {4: (7, 6), 5: (5, 4), 6: (1, 0, 3), 7: (2,)}
 DIAG_ORDER = sum(DIAG_WORK.values(), ())
 
 
@@ -71,11 +71,12 @@
     def pos(first_x, da, db):
         return (wrap(y + db), wrap(x + da)) if first_x else (wrap(y + da), wrap(x + db))
 
-    def plus_dir(is_x, t, src):
-        alt = lax.rem(t + src, 2) == 0
-        if is_x:
-            return alt
-        return where(src == 1, lax.rem(t, 3) != 0, alt)
+    def plus_first(t, src):
+        return lax.rem(t + src, 2) == 0
+
+    def plus_second(is_x, t, src, a):
+        alt = lax.rem(t, 2) == (0 if a in (0, 3) else 1)
+        return alt if is_x else where(src == 1, a != 2, alt)
 
     def neighbour(first_x, first_axis, d):
         on_x = first_x == first_axis
@@ -105,34 +106,42 @@
     def to_partner(first_x, r, i):
         c = group(r, first_x, i, k)
         pltpu.make_async_remote_copy(
-            src_ref=c, dst_ref=c, send_sem=send_sem.at[r, 5], recv_sem=par_sem.at[r, i],
+            src_ref=c, dst_ref=c, send_sem=send_sem.at[r, 3], recv_sem=par_sem.at[r, i],
             device_id=partner, device_id_type=MESH).start()
 
     def own_local(r):
         return where(r < DIAG, diag_main(r), (y < 2) | ((y == 2) & (r < DIAG + 8)))
 
-    def l_strip(strip):
-        return l_vm.at[pl.ds(pl.multiple_of(strip * blk, blk), blk), :]
+    def l_block(strip):
+        return l_ref.at[pl.ds(pl.multiple_of(strip * blk, blk), blk), :]
+
+    def own_strip(r):
+        return where(r < DIAG, per_row * y + diag_strip(r)[0], full_strip(r - DIAG, y)[0])
 
     def local_copy(r):
-        strip = where(r < DIAG, per_row * y + diag_strip(r)[0], full_strip(r - DIAG, y)[0])
-        return pltpu.make_async_copy(l_strip(strip), chunk(r, y, x, k), loc_sem.at[r])
+        return pltpu.make_async_copy(
+            l_vm.at[pl.ds(pl.multiple_of(own_strip(r) * blk, blk), blk), :], chunk(r, y, x, k), loc_sem.at[r])
 
     def inject(t):
         for first_x, r in slots(t):
             @pl.when(exists(r, k))
             def _():
+                def go(src):
+                    for first_axis in (True, False):
+                        for d in (1, -1):
+                            pltpu.make_async_remote_copy(
+                                src_ref=src, dst_ref=chunk(r, y, x, k), send_sem=send_sem.at[r, 0],
+                                recv_sem=osem(r, y, x), device_id=neighbour(first_x, first_axis, d),
+                                device_id_type=MESH).start()
+
                 @pl.when(own_local(r))
                 def _():
-                    local_copy(r).wait()
+                    go(l_block(own_strip(r)))
 
                 @pl.when(jnp.logical_not(own_local(r)))
                 def _():
                     wait_n(osem(r, y, x), 1)
-
-                for first_axis in (True, False):
-                    for d in (1, -1):
-                        rcopy(r, y, x, neighbour(first_x, first_axis, d), 0, osem(r, y, x)).start()
+                    go(chunk(r, y, x, k))
 
     def first_step(t, i):
         for first_x, r in slots(t):
@@ -142,33 +151,36 @@
             def _():
                 wait_n(osem(r, yy, xx), 1)
                 if i < 3:
-                    plus = plus_dir(first_x, t, xx if first_x else yy)
+                    plus = plus_first(t, xx if first_x else yy)
 
                     @pl.when(plus if i == 1 else jnp.logical_not(plus))
                     def _():
-                        rcopy(r, yy, xx, neighbour(first_x, True, 1 if i == 1 else -1), i, osem(r, yy, xx)).start()
+                        rcopy(r, yy, xx, neighbour(first_x, True, 1 if i == 1 else -1), 0, osem(r, yy, xx)).start()
                 for d in (1, -1):
                     rcopy(r, yy, xx, neighbour(first_x, False, d), 0, osem(r, yy, xx)).start()
                 if i == 3:
+                    @pl.when(own_local(r))
+                    def _():
+                        local_copy(r).wait()
                     to_partner(first_x, r, 0)
 
-    def second_step(t):
-        for i in (1, 2):
-            for first_x, r in slots(t):
-                @pl.when(exists(r, k))
-                def _():
-                    p0, q0 = pos(first_x, 0, OFFS[i])
-                    plus = plus_dir(not first_x, t, p0 if first_x else q0)
-                    fwd = plus if i == 1 else jnp.logical_not(plus)
-                    for a in range(4):
-                        yy, xx = pos(first_x, OFFS[a], OFFS[i])
-                        wait_n(osem(r, yy, xx), 1)
-
-                        @pl.when(fwd)
-                        def _():
-                            rcopy(r, yy, xx, neighbour(first_x, False, 1 if i == 1 else -1), 2 + i,
-                                  far_sem.at[r]).start()
-                    to_partner(first_x, r, i)
+    def second_src(first_x, i):
+        p0, q0 = pos(first_x, 0, OFFS[i])
+        return p0 if first_x else q0
+
+    def second_step(t, i):
+        for first_x, r in slots(t):
+            @pl.when(exists(r, k))
+            def _():
+                for a in range(4):
+                    yy, xx = pos(first_x, OFFS[a], OFFS[i])
+                    wait_n(osem(r, yy, xx), 1)
+                    plus = plus_second(not first_x, t, second_src(first_x, i), a)
+
+                    @pl.when(plus if i == 1 else jnp.logical_not(plus))
+                    def _():
+                        rcopy(r, yy, xx, neighbour(first_x, False, 1 if i == 1 else -1), i, far_sem.at[r]).start()
+                to_partner(first_x, r, i)
 
     def far_step(t):
         for first_x, r in slots(t):
@@ -181,26 +193,26 @@
         for first_x, r in slots(t):
             @pl.when(exists(r, k))
             def _():
-                wait_n(send_sem.at[r, 0], 10)
+                wait_n(send_sem.at[r, 0], 11)
                 for i in (1, 2):
-                    yy, xx = pos(first_x, OFFS[i], 0)
-                    plus = plus_dir(first_x, t, xx if first_x else yy)
-
-                    @pl.when(plus if i == 1 else jnp.logical_not(plus))
-                    def _():
-                        wait_n(send_sem.at[r, i], 1)
-                    yy, xx = pos(first_x, 0, OFFS[i])
-                    plus = plus_dir(not first_x, t, yy if first_x else xx)
-
-                    @pl.when(plus if i == 1 else jnp.logical_not(plus))
-                    def _():
-                        wait_n(send_sem.at[r, 2 + i], 4)
-                wait_n(send_sem.at[r, 5], 4 * side)
+                    if first_x:
+                        odd = second_src(first_x, i) == 1
+
+                        @pl.when(odd)
+                        def _():
+                            wait_n(send_sem.at[r, i], 3 if i == 1 else 1)
+
+                        @pl.when(jnp.logical_not(odd))
+                        def _():
+                            wait_n(send_sem.at[r, i], 2)
+                    else:
+                        wait_n(send_sem.at[r, i], 2)
+                wait_n(send_sem.at[r, 3], 4 * side)
 
     def fold_copy(f):
         r = DIAG + f
         return pltpu.make_async_remote_copy(
-            src_ref=l_strip(8 + f), dst_ref=chunk(r, 3 - y, x, k), send_sem=fold_sem.at[f],
+            src_ref=l_block(8 + f), dst_ref=chunk(r, 3 - y, x, k), send_sem=fold_sem.at[f],
             recv_sem=osem(r, 3 - y, x), device_id=dev(3 - y, x, k), device_id_type=MESH)
 
     def fold_cond(f):
@@ -208,7 +220,7 @@
 
     def xfold(r):
         return pltpu.make_async_remote_copy(
-            src_ref=l_strip(per_row * y + diag_strip(r)[1]), dst_ref=chunk(r, y, 3 - x, k),
+            src_ref=l_block(per_row * y + diag_strip(r)[1]), dst_ref=chunk(r, y, 3 - x, k),
             send_sem=xfold_sem.at[r], recv_sem=osem(r, y, 3 - x), device_id=dev(y, 3 - x, k), device_id_type=MESH)
 
     def xfold_cond(r):
@@ -266,9 +278,8 @@
             pltpu.make_async_copy(
                 g_ref.at[r, yy, m % 2, xx], st_d.at[buf, :, m * blk:(m + 1) * blk], std_sem.at[buf]).start()
 
-    def diag_compute(p):
+    def diag_compute(p, following):
         n = (p + 1) * blk
-        diag_stage(p, 0, 0)
 
         def one(yy, _):
             buf = lax.rem(yy, 2)
@@ -276,6 +287,10 @@
             @pl.when(yy + 1 < side)
             def _():
                 diag_stage(p, yy + 1, 1 - buf)
+            if following is not None:
+                @pl.when(yy + 1 == side)
+                def _():
+                    diag_stage(following, 0, 1 - buf)
             c = st_d.at[buf, :, pl.ds(0, n)]
             pltpu.make_async_copy(c, c, std_sem.at[buf]).wait()
             add_dot(st_d[buf, :, :n], yy * wide, n, per_row * yy + p)
@@ -305,10 +320,16 @@
     l_load = pltpu.make_async_copy(l_ref, l_vm, load_sem.at[0])
     l_load.start()
     b_load = pltpu.make_async_copy(b_ref, b_vm, load_sem.at[1])
-    b_load.start()
     barrier = pltpu.get_barrier_semaphore()
     for d in (dev(y, wrap(x + 1), k), dev(y, wrap(x - 1), k), dev(wrap(y + 1), x, k), dev(wrap(y - 1), x, k), partner):
         pl.semaphore_signal(barrier, inc=1, device_id=d, device_id_type=MESH)
+    pl.semaphore_wait(barrier, 5)
+    for r in (3, 4, 5):
+        @pl.when(xfold_cond(r))
+        def _():
+            xfold(r).start()
+    inject(0)
+    inject(1)
     l_load.wait()
 
     def start_local(r, _):
@@ -317,13 +338,7 @@
             local_copy(r).start()
         return 0
     lax.fori_loop(0, SLOTS, start_local, 0)
-    pl.semaphore_wait(barrier, 5)
-    for r in (3, 4, 5):
-        @pl.when(xfold_cond(r))
-        def _():
-            xfold(r).start()
-    inject(0)
-    inject(1)
+    b_load.start()
 
     def zero(i, _):
         acc[pl.ds(pl.multiple_of(i * blk, blk), blk), :] = jnp.zeros((blk, cols), acc.dtype)
@@ -337,95 +352,66 @@
 
     def body(n, _):
         t = n - 1
-        now = (t >= 0) & (t < PAIRS)
-        now_full = (t >= FULL_PAIR) & (t < PAIRS)
-        before = t >= 1
-        before_full = t > FULL_PAIR
-        after = t + 1 < PAIRS
-
-        @pl.when((t >= 0) & (t + 2 < PAIRS))
-        def _():
-            inject(t + 2)
-
-        @pl.when(t + 1 < FULL // 2)
-        def _():
-            for s in range(2):
-                f = 2 * (t + 1) + s
-
-                @pl.when(fold_cond(f))
-                def _():
-                    fold_copy(f).start()
-
-        @pl.when(after)
-        def _():
-            first_step(t + 1, 1)
-            first_step(t + 1, 2)
-
-        @pl.when(now)
-        def _():
-            second_step(t)
-
-        @pl.when(before)
-        def _():
-            far_step(t - 1)
-
-        @pl.when(now)
-        def _():
-            push(t, 1, 1)
-
-        @pl.when(now_full)
-        def _():
-            compute(t, 0, 0)
-
-        @pl.when(now)
-        def _():
-            push(t, 2, 0)
-
-        @pl.when(now_full)
-        def _():
-            compute(t, 1, 1)
-
-        @pl.when(after)
-        def _():
-            first_step(t + 1, 3)
-
-        @pl.when(before)
-        def _():
-            push(t - 1, 3, 1)
-
-        @pl.when(now_full)
-        def _():
-            compute(t, 2, 0)
-
-        @pl.when(after)
-        def _():
-            push(t + 1, 0, 0)
-
-        @pl.when(before_full)
-        def _():
-            compute(t - 1, 3, 1)
+
+        def on(u, fn, lo=0):
+            pl.when((u >= lo) & (u < PAIRS))(fn)
+
+        def full(u, fn):
+            on(u, fn, FULL_PAIR)
+
         for tt, ps in DIAG_WORK.items():
             @pl.when(t == tt)
             def _():
-                for p in ps:
-                    diag_compute(p)
+                diag_stage(ps[0], 0, 0)
+        on(t - 1, lambda: second_step(t - 1, 1))
+        on(t - 1, lambda: push(t - 1, 0, 0))
+        for tt, ps in DIAG_WORK.items():
+            @pl.when(t == tt)
+            def _():
+                for h, p in enumerate(ps):
+                    diag_compute(p, ps[h + 1] if h + 1 < len(ps) else None)
                     n_th = DIAG_ORDER.index(p)
                     if n_th:
                         out_copy(DIAG_ORDER[n_th - 1], 4, outd_sem.at[0]).wait()
                     put(p, 4, outd_sem.at[0])
-
-        @pl.when(before_full)
-        def _():
-            @pl.when(t > FULL_PAIR + 1)
-            def _():
-                emit_wait(t - 2)
-            emit(t - 1)
-
-        @pl.when(before)
-        def _():
-            drain(t - 1)
+        on(t - 2, lambda: far_step(t - 2))
+        full(t - 3, lambda: compute(t - 3, 3, 1))
+        on(t - 1, lambda: second_step(t - 1, 2))
+        on(t - 1, lambda: push(t - 1, 1, 1))
+        on(t, lambda: first_step(t, 3))
+
+        @pl.when((t >= 0) & (t + 2 < PAIRS))
+        def _():
+            inject(t + 2)
+
+        @pl.when(t + 1 < FULL // 2)
+        def _():
+            for h in range(2):
+                f = 2 * (t + 1) + h
+
+                @pl.when(fold_cond(f))
+                def _():
+                    fold_copy(f).start()
+        full(t - 1, lambda: compute(t - 1, 0, 0))
+
+        @pl.when(t + 1 < PAIRS)
+        def _():
+            first_step(t + 1, 1)
+            first_step(t + 1, 2)
+        on(t - 1, lambda: push(t - 1, 2, 0))
+        full(t - 1, lambda: compute(t - 1, 1, 1))
+        on(t - 2, lambda: push(t - 2, 3, 1))
+        full(t - 1, lambda: compute(t - 1, 2, 0))
+
+        def send_out():
+            @pl.when(t - 4 >= FULL_PAIR)
+            def _():
+                emit_wait(t - 4)
+            emit(t - 3)
+        full(t - 3, send_out)
+        on(t - 2, lambda: drain(t - 2))
         return 0
-    lax.fori_loop(0, PAIRS + 2, body, 0)
+    lax.fori_loop(0, PAIRS + 4, body, 0)
 
     def fold_drain(f, _):
         @pl.when(fold_cond(f))
@@ -465,7 +451,7 @@
                 dma((SLOTS, side * side)),
                 dma((SLOTS,)),
                 dma((SLOTS, 4)),
-                dma((SLOTS, 6)),
+                dma((SLOTS, 4)),
                 dma((SLOTS,)),
                 dma((FULL,)),
                 dma((DIAG,)),

time: 268 us -> 239 us (0.89)
  Pallas kernels: 253 us -> 223 us
    pallas_call x1, Pallas kernels: 253 us -> 223 us  [local_product(): pl.pallas_call(functools.partial(kernel, side), out_shape=(jax.ShapeDtype...]
where the time goes in v3:
time: 239 us; the launch traced here: 237 us
  Pallas kernels  223 us (93%)
  local copies, waits for them, and re-layouts  13.9 us (6%)
    pallas_call x1, Pallas kernels, local_product(): pl.pallas_call(functools.partial(kernel, side), out_shape=(jax.ShapeDtype...  223 us
    unnamed x1, local copies, waits for them, and re-layouts  13.9 us

profile of v3, /device:TPU:97, one launch (start us, length us, event | category | flops | bytes accessed | tf_op | source)
XLA Modules:
  0.0 236.7 jit_solution(4354457540328760464)
XLA Ops:
  0.0 222.7 %shard_map.28 = (bf16[8192,1024]{1,0:T(8,128)(2,1)}, bf16[18,4,2,4,256,256]{5,4,3,2,1,0:T(8,128)(2,1)}) custom-call(bf16[8192,256]{1,0:T(8,128)(2,1)} %l_ref.1, bf16[8192,1024]{1,0:T(8,128)(2,1)} %b_ref.1), custom_call_target="tpu_custom_call" | custom-call | flops 68719476736 | bytes 33554432 | tf_op jit(solution)/shard_map/pallas_call | solution.py:435
  222.8 13.9 %copy.4 = bf16[8192,1024]{1,0:T(8,128)(2,1)} copy(bf16[8192,1024]{1,0:T(8,128)(2,1)} %get-tuple-element.6) | data formatting | bytes 33554432

commit v4 on v3

--- a/solution.py
+++ b/solution.py
@@ -28,9 +28,24 @@
     return alt[p], 3 - h
 
 
-def kernel(side, l_ref, b_ref, y_ref, g_ref, b_vm, acc, l_vm, st_x, st_y, st_d, out_st,
+def full_strip(f, yy):
+    strip = jnp.where(yy < 2, 20 + f, jnp.where((yy == 2) & (f < 8), 24 + f, 8 + f))
+    grp = jnp.where(yy == 1, 1, jnp.where(yy == 2, jnp.where(f < 8, 2, 1), 0))
+    return strip, grp
+
+
+def strip_rows(ref, strip, blk):
+    return ref.at[pl.ds(pl.multiple_of(strip * blk, blk), blk), :]
+
+
+def late_strips(f, yy):
+    first = full_strip(f, yy)[0]
+    return (first, 21 + f, 9 + f), 28 + 2 * f - first
+
+
+def kernel(side, l_ref, b_ref, y_ref, part_ref, g_ref, b_vm, acc, l_vm, st_x, st_y, st_d, out_st,
            own_sem, far_sem, par_sem, send_sem, loc_sem, fold_sem, xfold_sem, load_sem,
-           stx_sem, sty_sem, std_sem, out_sem, outd_sem):
+           stx_sem, sty_sem, std_sem, out_sem, outd_sem, part_sem):
     rows, blk = l_ref.shape
     cols = b_ref.shape[1]
     per_row = 2 * side
@@ -48,11 +63,6 @@
         return {"col": (yy * side + xx) * 2 + kk}
 
     partner = dev(y, x, 1 - k)
-
-    def full_strip(f, yy):
-        strip = where(yy < 2, 20 + f, where((yy == 2) & (f < 8), 24 + f, 8 + f))
-        grp = where(yy == 1, 1, where(yy == 2, where(f < 8, 2, 1), 0))
-        return strip, grp
 
     def diag_main(r):
         return x < where(r <= 2, 4, where(r <= 4, 3, 2))
@@ -411,7 +421,19 @@
         full(t - 3, send_out)
         on(t - 2, lambda: drain(t - 2))
         return 0
-    lax.fori_loop(0, PAIRS + 4, body, 0)
+    lax.fori_loop(0, PAIRS + 2, body, 0)
+
+    last = PAIRS - 1
+    late, other = late_strips(2 * last - DIAG, wrap(y + OFFS[3]))
+    parts = [pltpu.make_async_copy(strip_rows(acc, v, blk), part_ref.at[h], part_sem.at[h]) for h, v in enumerate(late)]
+    for c in parts:
+        c.start()
+    out_copy(DIAG_ORDER[-1], 4, outd_sem.at[0]).wait()
+    put(other, 4, outd_sem.at[0])
+    compute(last - 1, 3, 1)
+    emit_wait(last - 2)
+    emit(last - 1)
+    far_step(last)
 
     def fold_drain(f, _):
         @pl.when(fold_cond(f))
@@ -419,8 +441,88 @@
             fold_copy(f).wait_send()
         return 0
     lax.fori_loop(0, FULL, fold_drain, 0)
-    emit_wait(PAIRS - 1)
-    out_copy(DIAG_ORDER[-1], 4, outd_sem.at[0]).wait()
+    for c in parts:
+        c.wait()
+    emit_wait(last - 1)
+    out_copy(other, 4, outd_sem.at[0]).wait()
+    par_wait(last, 3)
+    drain(last)
+
+
+def finish(side, y_ref, part_ref, g_ref, b_ref, x_ref, move, bx, by, gx, gy, pv, ov,
+           in_sem, read_sem, write_sem):
+    blk, cols = move.shape[1:]
+    n_copy = move.shape[0]
+    per_row = 2 * side
+    wide = per_row * blk
+    me = lax.axis_index("col")
+    x = lax.rem(me // 2, side)
+    y = me // per_row
+    yy = lax.rem(y + 2, side)
+    xx = lax.rem(x + 2, side)
+    r = SLOTS - 2
+    f = r - DIAG
+    late, other = late_strips(f, yy)
+    grp = full_strip(f, yy)[1]
+
+    loads = [pltpu.make_async_copy(part_ref, pv, in_sem.at[0]),
+             pltpu.make_async_copy(b_ref.at[pl.ds(pl.multiple_of(grp * wide, wide), wide), :], bx, in_sem.at[1])]
+    for h in range(2):
+        loads.append(pltpu.make_async_copy(
+            b_ref.at[pl.ds(pl.multiple_of(h * wide + xx * (2 * blk), 2 * blk), 2 * blk), :], by.at[h], in_sem.at[2 + h]))
+    for c in loads:
+        c.start()
+    for kk in range(2):
+        for j in range(side):
+            pltpu.make_async_copy(
+                g_ref.at[r, yy, kk, j], gx.at[:, (2 * j + kk) * blk:(2 * j + kk + 1) * blk], in_sem.at[4]).start()
+            pltpu.make_async_copy(
+                g_ref.at[r + 1, j, kk, xx], gy.at[j, :, kk * blk:(kk + 1) * blk], in_sem.at[5]).start()
+
+    def moved(i):
+        low = 8 + f
+        return jnp.where(i < low, i, jnp.where(i < n_copy - 1, i + 2, other))
+
+    def read(i):
+        return pltpu.make_async_copy(strip_rows(y_ref, moved(i), blk), move.at[i], read_sem.at[i])
+
+    def write(i):
+        return pltpu.make_async_copy(move.at[i], strip_rows(x_ref, moved(i), blk), write_sem.at[i])
+
+    def each(fn):
+        def step(i, _):
+            fn(i)
+            return 0
+        lax.fori_loop(0, n_copy, step, 0)
+
+    each(lambda i: read(i).start())
+    for c in loads:
+        c.wait()
+    pltpu.make_async_copy(gx, gx, in_sem.at[4]).wait()
+    pltpu.make_async_copy(gy, gy, in_sem.at[5]).wait()
+    wn = min(256, cols)
+
+    def dot(lhs, rhs):
+        return jnp.dot(lhs, rhs, preferred_element_type=jnp.float32)
+
+    out = [pltpu.make_async_copy(ov.at[h], strip_rows(x_ref, late[h], blk), write_sem.at[n_copy + h]) for h in range(3)]
+    for n in range(cols // wn):
+        c = slice(n * wn, (n + 1) * wn)
+        ov[0, :, c] = (pv[0, :, c] + dot(gx[...], bx[:, c])).astype(ov.dtype)
+    out[0].start()
+    for h, rows in ((1, ((0, 0), (1, 1))), (2, ((2, 1), (3, 0)))):
+        for n in range(cols // wn):
+            c = slice(n * wn, (n + 1) * wn)
+            ov[h, :, c] = (pv[h, :, c] + sum(dot(gy[a], by[g, :, c]) for a, g in rows)).astype(ov.dtype)
+        out[h].start()
+
+    def pass_on(i):
+        read(i).wait()
+        write(i).start()
+    each(pass_on)
+    each(lambda i: write(i).wait())
+    for c in out:
+        c.wait()
 
 
 def solution(mesh):
@@ -432,14 +534,17 @@
         cols = b_cols.shape[1]
         per_row = 2 * side
         dma = pltpu.SemaphoreType.DMA
-        product, _ = pl.pallas_call(
+        n_copy = rows // blk - 3
+        params = pltpu.CompilerParams(collective_id=0, has_side_effects=True, vmem_limit_bytes=67043328)
+        strips, partial, gathered = pl.pallas_call(
             functools.partial(kernel, side),
             out_shape=(
                 jax.ShapeDtypeStruct((rows, cols), jnp.bfloat16),
+                jax.ShapeDtypeStruct((3, blk, cols), jnp.float32),
                 jax.ShapeDtypeStruct((SLOTS, side, 2, side, blk, blk), jnp.bfloat16),
             ),
             in_specs=[pl.BlockSpec(memory_space=pl.ANY)] * 2,
-            out_specs=(pl.BlockSpec(memory_space=pl.ANY),) * 2,
+            out_specs=(pl.BlockSpec(memory_space=pl.ANY),) * 3,
             scratch_shapes=[
                 pltpu.VMEM((rows, cols), jnp.bfloat16),
                 pltpu.VMEM((rows, cols), jnp.float32),
@@ -461,11 +566,30 @@
                 dma((2,)),
                 dma((4,)),
                 dma((1,)),
+                dma((3,)),
             ],
-            compiler_params=pltpu.CompilerParams(
-                collective_id=0, has_side_effects=True, vmem_limit_bytes=67043328),
+            compiler_params=params,
             cost_estimate=pl.CostEstimate(flops=rows * rows * cols, bytes_accessed=4 * rows * cols, transcendentals=0),
         )(l_cols, b_cols)
-        return product
+        return pl.pallas_call(
+            functools.partial(finish, side),
+            out_shape=jax.ShapeDtypeStruct((rows, cols), jnp.bfloat16),
+            in_specs=[pl.BlockSpec(memory_space=pl.ANY)] * 4,
+            out_specs=pl.BlockSpec(memory_space=pl.ANY),
+            scratch_shapes=[
+                pltpu.VMEM((n_copy, blk, cols), jnp.bfloat16),
+                pltpu.VMEM((per_row * blk, cols), jnp.bfloat16),
+                pltpu.VMEM((2, 2 * blk, cols), jnp.bfloat16),
+                pltpu.VMEM((blk, per_row * blk), jnp.bfloat16),
+                pltpu.VMEM((side, blk, 2 * blk), jnp.bfloat16),
+                pltpu.VMEM((3, blk, cols), jnp.float32),
+                pltpu.VMEM((3, blk, cols), jnp.bfloat16),
+                dma((6,)),
+                dma((n_copy,)),
+                dma((n_copy + 3,)),
+            ],
+            compiler_params=pltpu.CompilerParams(vmem_limit_bytes=67043328),
+            cost_estimate=pl.CostEstimate(flops=2 * rows * blk * cols, bytes_accessed=6 * rows * cols, transcendentals=0),
+        )(strips, partial, gathered, b_cols)
 
     return jax.shard_map(local_product, mesh=mesh, in_specs=(P("batch", "col"), P("batch", "col")), out_specs=P("batch", "col"), check_vma=False)

time: 239 us -> 236 us (0.987); the launches traced: 237 us -> 231 us
  local copies, waits for them, and re-layouts: 13.9 us -> 0 us
  Pallas kernels: 223 us -> 231 us
    unnamed x1 -> x0, local copies, waits for them, and re-layouts: 13.9 us -> none
    pallas_call x0 -> x1, Pallas kernels: none -> 13.9 us  [local_product(): pl.pallas_call(functools.partial(finish, side), out_shape=jax.ShapeDtypeS...]
    pallas_call x1, Pallas kernels: 223 us -> 217 us  [local_product(): pl.pallas_call(functools.partial(kernel, side), out_shape=(jax.ShapeDtype...]
where the time goes in v4:
time: 236 us; the launch traced here: 231 us
  Pallas kernels  231 us (98%)
    pallas_call x1, Pallas kernels, local_product(): pl.pallas_call(functools.partial(kernel, side), out_shape=(jax.ShapeDtype...  217 us
    pallas_call x1, Pallas kernels, local_product(): pl.pallas_call(functools.partial(finish, side), out_shape=jax.ShapeDtypeS...  13.9 us

profile of v4, /device:TPU:97, one launch (start us, length us, event | category | flops | bytes accessed | tf_op | source)
XLA Modules:
  0.0 231.2 jit_solution(14777564724508522913)
XLA Ops:
  0.0 217.1 %shard_map.28 = (bf16[8192,1024]{1,0:T(8,128)(2,1)}, f32[3,256,1024]{2,1,0:T(8,128)}, bf16[18,4,2,4,256,256]{5,4,3,2,1,0:T(8,128)(2,1)}) custom-call(bf16[8192,256]{1,0:T(8,128)(2,1)} %l_ref.1, bf16[8192,1024]{1,0:T(8,128)(2,1)} %b_ref.3), custom_call_target="tpu_custom_call" | custom-call | flops 68719476736 | bytes 33554432 | tf_op jit(solution)/shard_map/pallas_call | solution.py:539
  217.1 13.9 %shard_map.29 = bf16[8192,1024]{1,0:T(8,128)(2,1)} custom-call(bf16[8192,1024]{1,0:T(8,128)(2,1)} %get-tuple-element.8.y_ref, f32[3,256,1024]{2,1,0:T(8,128)} %get-tuple-element.9.part_ref, bf16[18,4,2,4,256,256]{5,4,3,2,1,0:T(8,128)(2,1)} %get-tuple-element.10.g_ref, bf16[8192,1024]{1,0:T(8,128)(2,1)} %b_ref.3), custom_call_target="tpu_custom_call" | custom-call | flops 4294967296 | bytes 50331648 | tf_op jit(solution)/shard_map/pallas_call | solution.py:574

commit v5 on v3

--- a/solution.py
+++ b/solution.py
@@ -28,9 +28,23 @@
     return alt[p], 3 - h
 
 
-def kernel(side, l_ref, b_ref, y_ref, g_ref, b_vm, acc, l_vm, st_x, st_y, st_d, out_st,
+def full_strip(f, yy):
+    strip = jnp.where(yy < 2, 20 + f, jnp.where((yy == 2) & (f < 8), 24 + f, 8 + f))
+    grp = jnp.where(yy == 1, 1, jnp.where(yy == 2, jnp.where(f < 8, 2, 1), 0))
+    return strip, grp
+
+
+def strip_rows(ref, strip, blk):
+    return ref.at[pl.ds(pl.multiple_of(strip * blk, blk), blk), :]
+
+
+LATE = FULL - 2
+LATE_STRIPS = (20 + LATE, 8 + LATE, 21 + LATE, 9 + LATE)
+
+
+def kernel(side, l_ref, b_ref, y_ref, part_ref, g_ref, b_vm, acc, l_vm, st_x, st_y, st_d, out_st,
            own_sem, far_sem, par_sem, send_sem, loc_sem, fold_sem, xfold_sem, load_sem,
-           stx_sem, sty_sem, std_sem, out_sem, outd_sem):
+           stx_sem, sty_sem, std_sem, out_sem, outd_sem, part_sem):
     rows, blk = l_ref.shape
     cols = b_ref.shape[1]
     per_row = 2 * side
@@ -48,11 +62,6 @@
         return {"col": (yy * side + xx) * 2 + kk}
 
     partner = dev(y, x, 1 - k)
-
-    def full_strip(f, yy):
-        strip = where(yy < 2, 20 + f, where((yy == 2) & (f < 8), 24 + f, 8 + f))
-        grp = where(yy == 1, 1, where(yy == 2, where(f < 8, 2, 1), 0))
-        return strip, grp
 
     def diag_main(r):
         return x < where(r <= 2, 4, where(r <= 4, 3, 2))
@@ -247,7 +256,7 @@
     def push(t, i, buf):
         par_wait(t, i)
 
-        @pl.when(t >= FULL_PAIR)
+        @pl.when((t >= FULL_PAIR) & (t < PAIRS - 1))
         def _():
             stage(t, i, buf)
 
@@ -357,7 +366,7 @@
             pl.when((u >= lo) & (u < PAIRS))(fn)
 
         def full(u, fn):
-            on(u, fn, FULL_PAIR)
+            pl.when((u >= FULL_PAIR) & (u < PAIRS - 1))(fn)
 
         for tt, ps in DIAG_WORK.items():
             @pl.when(t == tt)
@@ -411,7 +420,17 @@
         full(t - 3, send_out)
         on(t - 2, lambda: drain(t - 2))
         return 0
-    lax.fori_loop(0, PAIRS + 4, body, 0)
+    lax.fori_loop(0, PAIRS + 2, body, 0)
+
+    last = PAIRS - 1
+    parts = [pltpu.make_async_copy(strip_rows(acc, v, blk), part_ref.at[h], part_sem.at[h]) for h, v in enumerate(LATE_STRIPS)]
+    for c in parts:
+        c.start()
+    out_copy(DIAG_ORDER[-1], 4, outd_sem.at[0]).wait()
+    compute(last - 1, 3, 1)
+    emit_wait(last - 2)
+    emit(last - 1)
+    far_step(last)
 
     def fold_drain(f, _):
         @pl.when(fold_cond(f))
@@ -419,8 +438,83 @@
             fold_copy(f).wait_send()
         return 0
     lax.fori_loop(0, FULL, fold_drain, 0)
-    emit_wait(PAIRS - 1)
-    out_copy(DIAG_ORDER[-1], 4, outd_sem.at[0]).wait()
+    for c in parts:
+        c.wait()
+    emit_wait(last - 1)
+    par_wait(last, 3)
+    drain(last)
+
+
+def finish(side, y_ref, part_ref, g_ref, b_ref, x_ref, move, bv, gv, pv, ov,
+           b_sem, g_sem, p_sem, read_sem, write_sem):
+    blk, cols = move.shape[1:]
+    n_copy = move.shape[0]
+    wide = 2 * side * blk
+    wn = min(256, cols)
+    terms = (((0, 0, 0), (1, 0, 3), (2, 1, 0), (3, 1, 3)), ((0, 0, 1), (1, 0, 2), (2, 1, 1), (3, 1, 2)))
+
+    def load_b(g):
+        return pltpu.make_async_copy(b_ref.at[pl.ds(g * wide, wide), :], bv.at[g], b_sem.at[g])
+
+    def load_p(h):
+        return pltpu.make_async_copy(part_ref.at[h], pv.at[h], p_sem.at[h])
+
+    def moved(i):
+        return jnp.where(i < LATE_STRIPS[1], i, i + 2)
+
+    def read(i):
+        return pltpu.make_async_copy(strip_rows(y_ref, moved(i), blk), move.at[i], read_sem.at[i])
+
+    def write(i):
+        return pltpu.make_async_copy(move.at[i], strip_rows(x_ref, moved(i), blk), write_sem.at[i])
+
+    def each(lo, hi, fn):
+        def step(i, _):
+            fn(i)
+            return 0
+        lax.fori_loop(lo, hi, step, 0)
+
+    per = -(-n_copy // 8)
+    n = 0
+    for g in range(2):
+        load_b(g).start()
+        for h, slot, yy in terms[g]:
+            for kk in range(2):
+                for j in range(side):
+                    pltpu.make_async_copy(
+                        g_ref.at[SLOTS - 2 + slot, yy, kk, j],
+                        gv.at[4 * g + h, :, (2 * j + kk) * blk:(2 * j + kk + 1) * blk], g_sem.at[4 * g + h]).start()
+            if g == 0:
+                load_p(h).start()
+            each(n, min(n + per, n_copy), lambda i: read(i).start())
+            n = min(n + per, n_copy)
+
+    def pass_on(i):
+        read(i).wait()
+        write(i).start()
+
+    n = 0
+    for g in range(2):
+        load_b(g).wait()
+        for h, _, _ in terms[g]:
+            c = gv.at[4 * g + h]
+            pltpu.make_async_copy(c, c, g_sem.at[4 * g + h]).wait()
+            if g == 0:
+                load_p(h).wait()
+            for m in range(cols // wn):
+                c = slice(m * wn, (m + 1) * wn)
+                total = pv[h, :, c] + jnp.dot(gv[4 * g + h], bv[g, :, c], preferred_element_type=jnp.float32)
+                if g == 0:
+                    pv[h, :, c] = total
+                else:
+                    ov[h, :, c] = total.astype(ov.dtype)
+            if g == 1:
+                pltpu.make_async_copy(ov.at[h], strip_rows(x_ref, LATE_STRIPS[h], blk), write_sem.at[n_copy + h]).start()
+            each(n, min(n + per, n_copy), pass_on)
+            n = min(n + per, n_copy)
+    each(0, n_copy, lambda i: write(i).wait())
+    for h in range(4):
+        pltpu.make_async_copy(ov.at[h], strip_rows(x_ref, LATE_STRIPS[h], blk), write_sem.at[n_copy + h]).wait()
 
 
 def solution(mesh):
@@ -432,14 +526,17 @@
         cols = b_cols.shape[1]
         per_row = 2 * side
         dma = pltpu.SemaphoreType.DMA
-        product, _ = pl.pallas_call(
+        n_copy = rows // blk - 4
+        params = pltpu.CompilerParams(collective_id=0, has_side_effects=True, vmem_limit_bytes=67043328)
+        strips, partial, gathered = pl.pallas_call(
             functools.partial(kernel, side),
             out_shape=(
                 jax.ShapeDtypeStruct((rows, cols), jnp.bfloat16),
+                jax.ShapeDtypeStruct((4, blk, cols), jnp.float32),
                 jax.ShapeDtypeStruct((SLOTS, side, 2, side, blk, blk), jnp.bfloat16),
             ),
             in_specs=[pl.BlockSpec(memory_space=pl.ANY)] * 2,
-            out_specs=(pl.BlockSpec(memory_space=pl.ANY),) * 2,
+            out_specs=(pl.BlockSpec(memory_space=pl.ANY),) * 3,
             scratch_shapes=[
                 pltpu.VMEM((rows, cols), jnp.bfloat16),
                 pltpu.VMEM((rows, cols), jnp.float32),
@@ -461,11 +558,30 @@
                 dma((2,)),
                 dma((4,)),
                 dma((1,)),
+                dma((4,)),
             ],
-            compiler_params=pltpu.CompilerParams(
-                collective_id=0, has_side_effects=True, vmem_limit_bytes=67043328),
+            compiler_params=params,
             cost_estimate=pl.CostEstimate(flops=rows * rows * cols, bytes_accessed=4 * rows * cols, transcendentals=0),
         )(l_cols, b_cols)
-        return product
+        return pl.pallas_call(
+            functools.partial(finish, side),
+            out_shape=jax.ShapeDtypeStruct((rows, cols), jnp.bfloat16),
+            in_specs=[pl.BlockSpec(memory_space=pl.ANY)] * 4,
+            out_specs=pl.BlockSpec(memory_space=pl.ANY),
+            scratch_shapes=[
+                pltpu.VMEM((n_copy, blk, cols), jnp.bfloat16),
+                pltpu.VMEM((2, per_row * blk, cols), jnp.bfloat16),
+                pltpu.VMEM((8, blk, per_row * blk), jnp.bfloat16),
+                pltpu.VMEM((4, blk, cols), jnp.float32),
+                pltpu.VMEM((4, blk, cols), jnp.bfloat16),
+                dma((2,)),
+                dma((8,)),
+                dma((4,)),
+                dma((n_copy,)),
+                dma((n_copy + 4,)),
+            ],
+            compiler_params=pltpu.CompilerParams(vmem_limit_bytes=67043328),
+            cost_estimate=pl.CostEstimate(flops=2 * rows * blk * cols, bytes_accessed=6 * rows * cols, transcendentals=0),
+        )(strips, partial, gathered, b_cols)
 
     return jax.shard_map(local_product, mesh=mesh, in_specs=(P("batch", "col"), P("batch", "col")), out_specs=P("batch", "col"), check_vma=False)

time: 239 us -> 237 us (level)
  local copies, waits for them, and re-layouts: 13.9 us -> 0 us
  Pallas kernels: 223 us -> 235 us
    pallas_call x0 -> x1, Pallas kernels: none -> 18.2 us  [local_product(): pl.pallas_call(functools.partial(finish, side), out_shape=jax.ShapeDtypeS...]
    unnamed x1 -> x0, local copies, waits for them, and re-layouts: 13.9 us -> none
    pallas_call x1, Pallas kernels: 223 us -> 216 us  [local_product(): pl.pallas_call(functools.partial(kernel, side), out_shape=(jax.ShapeDtype...]
where the time goes in v5:
time: 237 us; the launch traced here: 235 us
  Pallas kernels  235 us (99%)
    pallas_call x1, Pallas kernels, local_product(): pl.pallas_call(functools.partial(kernel, side), out_shape=(jax.ShapeDtype...  216 us
    pallas_call x1, Pallas kernels, local_product(): pl.pallas_call(functools.partial(finish, side), out_shape=jax.ShapeDtypeS...  18.2 us

profile of v5, /device:TPU:97, one launch (start us, length us, event | category | flops | bytes accessed | tf_op | source)
XLA Modules:
  0.0 234.8 jit_solution(15327495220304964167)
XLA Ops:
  0.0 216.4 %shard_map.28 = (bf16[8192,1024]{1,0:T(8,128)(2,1)}, f32[4,256,1024]{2,1,0:T(8,128)}, bf16[18,4,2,4,256,256]{5,4,3,2,1,0:T(8,128)(2,1)}) custom-call(bf16[8192,256]{1,0:T(8,128)(2,1)} %l_ref.1, bf16[8192,1024]{1,0:T(8,128)(2,1)} %b_ref.3), custom_call_target="tpu_custom_call" | custom-call | flops 68719476736 | bytes 33554432 | tf_op jit(solution)/shard_map/pallas_call | solution.py:531
  216.4 18.2 %shard_map.29 = bf16[8192,1024]{1,0:T(8,128)(2,1)} custom-call(bf16[8192,1024]{1,0:T(8,128)(2,1)} %get-tuple-element.8.y_ref, f32[4,256,1024]{2,1,0:T(8,128)} %get-tuple-element.9.part_ref, bf16[18,4,2,4,256,256]{5,4,3,2,1,0:T(8,128)(2,1)} %get-tuple-element.10.g_ref, bf16[8192,1024]{1,0:T(8,128)(2,1)} %b_ref.3), custom_call_target="tpu_custom_call" | custom-call | flops 4294967296 | bytes 50331648 | tf_op jit(solution)/shard_map/pallas_call | solution.py:566
